TPU v7x, 128 devices: a whole 4x4x4 slice. The times are simulated.
128 devices in a mesh: seq: 32 (over y, z, core), batch: 4 (over x).
Axes of the slice: x: 4, y: 4, z: 4, core: 2. Of those that a mesh axis runs over, the one named last changes fastest.
Arguments:
- queries: bfloat16 [4, 4096, 4096], P('batch', 'seq'), may hold values from -130 to 130
- keys: bfloat16 [4, 4096, 1024], P('batch', 'seq'), may hold values from -4 to 4
- values: bfloat16 [4, 4096, 1024], P('batch', 'seq'), may hold values from -4 to 4
- lengths: int32 [4], P('batch'), may hold values from 2048 to 4096
- block_pos: int32 [4, 32], P('batch'), may hold values from 0 to 31, each once within a row
- w_in: bfloat16 [6144, 1024], replicated, may hold values from -0.078125 to 0.078125
- b_in: float32 [1024], replicated, may hold values from -3 to 3
- output_weight: bfloat16 [1024, 8], replicated, may hold values from -0.1875 to 0.1875
- output_bias: float32 [8], replicated, may hold values from 1 to 2
Outputs:
- grad_w_in: float32 [6144, 1024], P(('seq', 'batch'))
- grad_b_in: float32 [1024], replicated
- output_weight_gradient: float32 [1024, 8], replicated
- output_bias_gradient: float32 [8], replicated
Inputs may be any that keep to these rules, and one draw needn't show every extreme that they name: Each row of block_pos names every block 0 to 31 once.
All inputs are finite; a program needn't handle non-finite values.
Results may differ from a plain program's by a relative error of at most 0.0017.
The roundings to bfloat16 on the way count: a program that leaves them out, or rounds other values in their place, can miss the bound.
Values may be sent and summed in bfloat16 or wider, within the bound.
No kernel may reach another device: no remote copies, remote signals or barrier semaphores. Data moves between devices by JAX's collectives and lax.ppermute only.
A program may use at most 128 MiB of HBM per device.

v0:
```python
import math
import jax
import jax.numpy as jnp
from jax import lax
from jax.sharding import PartitionSpec as P


def split_up(array, dim, size):
    before, after = (array.shape[:dim], array.shape[dim + 1 :])
    return jnp.moveaxis(array.reshape(*before, size, -1, *after), dim, 0)


def sent_and_summed(array, axis, dim):
    size = lax.axis_size(axis)
    tiles = lax.all_to_all(split_up(array, dim, size), axis, 0, 0, tiled=True)
    return jnp.sum(tiles, axis=0)


def in_one(arrays, axis):
    ends = [0]
    for a in arrays:
        ends.append(ends[-1] + a.size)
    so_far = lax.psum(jnp.concatenate([a.ravel() for a in arrays]), axis)
    return tuple((so_far[b:e].reshape(a.shape) for a, b, e in zip(arrays, ends, ends[1:])))


def on_device(queries, keys, values, lengths, block_pos, w_in, b_in, output_weight, output_bias):
    q_rows = queries[0]
    k_rows = keys[0]
    v_rows = values[0]
    rows = q_rows.shape[0]
    heads_kv = output_weight.shape[1]
    head_size = k_rows.shape[1] // heads_kv
    group_index = q_rows.shape[1] // k_rows.shape[1]
    scale = 1.0 / math.sqrt(head_size)
    every_key = lax.all_gather(k_rows, "seq", axis=0, tiled=True)
    total = every_key.shape[0]
    order = block_pos[0]
    offsets = jnp.arange(rows, dtype=jnp.int32)
    key_pos = (order[:, None] * rows + offsets[None, :]).reshape(-1)
    mine = lax.axis_index("seq")
    query_pos = lax.dynamic_index_in_dim(order, mine, 0, keepdims=False) * rows + offsets
    limit = lengths[0]
    allowed = (key_pos[None, :] <= query_pos[:, None]) & (key_pos < limit)[None, :]
    query_live = (query_pos < limit).astype(jnp.float32)

    def group_mass(index, sums):
        q_part = lax.dynamic_slice_in_dim(
            q_rows, index * group_index * head_size, group_index * head_size, 1
        )
        q_part = q_part.reshape(rows, group_index, head_size)
        k_part = lax.dynamic_slice_in_dim(every_key, index * head_size, head_size, 1)
        scores = (
            jnp.einsum("qhd,kd->hqk", q_part, k_part, preferred_element_type=jnp.float32) * scale
        )
        masked = jnp.where(allowed[None], scores, -1e30)
        top = jnp.max(masked, axis=2, keepdims=True)
        weights = jnp.where(allowed[None], jnp.exp(masked - top), 0.0)
        denom = jnp.sum(weights, axis=2, keepdims=True)
        share = weights / denom * query_live[None, :, None]
        column = jnp.sum(share, axis=(0, 1))
        return lax.dynamic_update_index_in_dim(sums, column, index, 0)

    partial_value = lax.fori_loop(
        0, heads_kv, group_mass, jnp.zeros((heads_kv, total), jnp.float32)
    )
    mass = sent_and_summed(partial_value, "seq", 1)
    labels = jnp.log1p(mass).T
    features = jnp.concatenate([q_rows, k_rows, v_rows], axis=1)
    pre = jnp.dot(features, w_in, preferred_element_type=jnp.float32) + b_in
    act = jax.nn.silu(pre).astype(jnp.bfloat16)
    pred = jnp.dot(act, output_weight, preferred_element_type=jnp.float32) + output_bias
    norm = 1.0 / math.sqrt(lax.axis_size("batch") * total)
    resid = ((pred - labels) * query_live[:, None] * norm).astype(jnp.bfloat16)
    back = lax.dot_general(
        resid, output_weight, (((1,), (1,)), ((), ())), preferred_element_type=jnp.float32
    )
    sig = jax.nn.sigmoid(pre)
    delta = (back * sig * (1.0 + pre * (1.0 - sig))).astype(jnp.bfloat16)
    out_term = lax.dot_general(
        act, resid, (((0,), (0,)), ((), ())), preferred_element_type=jnp.float32
    )
    grad_b_in, output_weight_gradient, output_bias_gradient = in_one(
        (
            jnp.sum(delta.astype(jnp.float32), axis=0),
            out_term,
            jnp.sum(resid.astype(jnp.float32), axis=0),
        ),
        ("seq", "batch"),
    )
    grad_w_in = lax.psum_scatter(
        lax.dot_general(
            features, delta, (((0,), (0,)), ((), ())), preferred_element_type=jnp.float32
        ),
        ("seq", "batch"),
        scatter_dimension=0,
        tiled=True,
    )
    return (grad_w_in, grad_b_in, output_weight_gradient, output_bias_gradient)


def solution(mesh):
    return jax.shard_map(
        on_device,
        mesh=mesh,
        in_specs=(
            P("batch", "seq", None),
            P("batch", "seq", None),
            P("batch", "seq", None),
            P("batch"),
            P("batch", None),
            P(),
            P(),
            P(),
            P(),
        ),
        out_specs=(P(("seq", "batch"), None), P(), P(), P()),
        check_vma=False,
    )
```

profile of v0, /device:TPU:0, one launch (start us, length us, event | category | flops | bytes accessed | tf_op | source)
XLA Modules:
  0.0 518.8 jit_solution(12301234503528148574)
XLA Ops:
  7.2 0.7 all-gather.3.cloned.1.call-update
  7.9 1.1 copy.15
  9.7 1.1 copy.16
  10.8 1.6 copy.14
  12.5 1.2 fusion.51
  13.7 0.6 iota_add_fusion
  14.4 0.7 multiply_bitcast_fusion
  15.2 50.5 %all-gather.3.cloned.1.call-done = bf16[1,4096,1024]{2,1,0:T(8,128)(2,1)} async-done(((bf16[1,128,1024]{2,1,0:T(8,128)(2,1)}), bf16[1,4096,1024]{2,1,0:T(8,128)(2,1)}) %all-gather.3.cloned.1.call-update) | async-done | bytes 8388624 | tf_op jit(solution)/shard_map/all_gather | solution.py:36
  65.7 170.6 %while.16 = (s32[]{:T(128)}, f32[8,4096]{1,0:T(8,128)}, bf16[4096,1024]{1,0:T(8,128)(2,1)}, bf16[128,4096]{0,1:T(8,128)(2,1)S(1)}, s32[128]{0:T(128)S(1)}, /*ind...) while((s32[]{:T(128)}, f32[8,4096]{1,0:T(8,128)}, ...), condition=%wide.region_4.5_spmd.clone, body=%wide.region_0.4_spmd.clone.sunk | while | flops 1097869184 | bytes 22091528 | solution.py:64
  65.7 1.3 compare_convert_fusion.3
  67.0 1.4 compare_and_fusion.2
  68.4 8.6 %fusion.72 = f32[4,128,4096]{1,2,0:T(8,128)} fusion(pred[128,4096]{0,1:T(8,128)(4,1)S(1)} %compare_and_fusion.2, bf16[128,4,128]{0,2,1:T(8,128)(2,1)S(1)} %bitcast.69, bf16[4096,1024]{1,0:T(8,128)(2,1)} %get-tuple-element.300, s32[]{:T(128)S(6)} %select_n.79), kind=kOutput, calls=%fused_computation.2.clone.1 | convolution fusion | flops 545268736 | bytes 10616836 | tf_op jit(solution)/shard_map/while/body/eval_jaxpr/div | solution.py:60
  77.0 8.4 %multiply_reduce_fusion.2 = f32[4096]{0:T(1024)S(1)} fusion(f32[4,128,4096]{1,2,0:T(8,128)} %fusion.72, f32[128]{0:T(128)S(1)} %compare_convert_fusion.3, pred[128,4096]{0,1:T(8,128)(4,1)S(1)} %compare_and_fusion.2, bf16[128,4,128]{0,2,1:T(8,128)(2,1)S(1)} %bitcast.70, bf16[4096,1024]{1,0:T(8,128)(2,1)} %get-tuple-element.300, s32[]{:T(128)S(6)} %select_n.79), kind=kOutput, calls=%fused_computation.5.clone.1 | convolution fusion | flops 551551488 | bytes 10633732 | tf_op jit(solution)/shard_map/while/body/eval_jaxpr/sub | solution.py:58
  85.4 1.6 dynamic_update_slice.13
  87.0 1.3 compare_convert_fusion.3
  88.3 1.4 compare_and_fusion.2
  89.7 8.6 %fusion.72 = f32[4,128,4096]{1,2,0:T(8,128)} fusion(pred[128,4096]{0,1:T(8,128)(4,1)S(1)} %compare_and_fusion.2, bf16[128,4,128]{0,2,1:T(8,128)(2,1)S(1)} %bitcast.69, bf16[4096,1024]{1,0:T(8,128)(2,1)} %get-tuple-element.300, s32[]{:T(128)S(6)} %select_n.79), kind=kOutput, calls=%fused_computation.2.clone.1 | convolution fusion | flops 545268736 | bytes 10616836 | tf_op jit(solution)/shard_map/while/body/eval_jaxpr/div | solution.py:60
  98.3 8.4 %multiply_reduce_fusion.2 = f32[4096]{0:T(1024)S(1)} fusion(f32[4,128,4096]{1,2,0:T(8,128)} %fusion.72, f32[128]{0:T(128)S(1)} %compare_convert_fusion.3, pred[128,4096]{0,1:T(8,128)(4,1)S(1)} %compare_and_fusion.2, bf16[128,4,128]{0,2,1:T(8,128)(2,1)S(1)} %bitcast.70, bf16[4096,1024]{1,0:T(8,128)(2,1)} %get-tuple-element.300, s32[]{:T(128)S(6)} %select_n.79), kind=kOutput, calls=%fused_computation.5.clone.1 | convolution fusion | flops 551551488 | bytes 10633732 | tf_op jit(solution)/shard_map/while/body/eval_jaxpr/sub | solution.py:58
  106.7 1.6 dynamic_update_slice.13
  108.3 1.3 compare_convert_fusion.3
  109.6 1.4 compare_and_fusion.2
  111.0 8.6 %fusion.72 = f32[4,128,4096]{1,2,0:T(8,128)} fusion(pred[128,4096]{0,1:T(8,128)(4,1)S(1)} %compare_and_fusion.2, bf16[128,4,128]{0,2,1:T(8,128)(2,1)S(1)} %bitcast.69, bf16[4096,1024]{1,0:T(8,128)(2,1)} %get-tuple-element.300, s32[]{:T(128)S(6)} %select_n.79), kind=kOutput, calls=%fused_computation.2.clone.1 | convolution fusion | flops 545268736 | bytes 10616836 | tf_op jit(solution)/shard_map/while/body/eval_jaxpr/div | solution.py:60
  119.6 8.4 %multiply_reduce_fusion.2 = f32[4096]{0:T(1024)S(1)} fusion(f32[4,128,4096]{1,2,0:T(8,128)} %fusion.72, f32[128]{0:T(128)S(1)} %compare_convert_fusion.3, pred[128,4096]{0,1:T(8,128)(4,1)S(1)} %compare_and_fusion.2, bf16[128,4,128]{0,2,1:T(8,128)(2,1)S(1)} %bitcast.70, bf16[4096,1024]{1,0:T(8,128)(2,1)} %get-tuple-element.300, s32[]{:T(128)S(6)} %select_n.79), kind=kOutput, calls=%fused_computation.5.clone.1 | convolution fusion | flops 551551488 | bytes 10633732 | tf_op jit(solution)/shard_map/while/body/eval_jaxpr/sub | solution.py:58
  128.0 1.6 dynamic_update_slice.13
  129.6 1.3 compare_convert_fusion.3
  131.0 1.4 compare_and_fusion.2
  132.4 8.6 %fusion.72 = f32[4,128,4096]{1,2,0:T(8,128)} fusion(pred[128,4096]{0,1:T(8,128)(4,1)S(1)} %compare_and_fusion.2, bf16[128,4,128]{0,2,1:T(8,128)(2,1)S(1)} %bitcast.69, bf16[4096,1024]{1,0:T(8,128)(2,1)} %get-tuple-element.300, s32[]{:T(128)S(6)} %select_n.79), kind=kOutput, calls=%fused_computation.2.clone.1 | convolution fusion | flops 545268736 | bytes 10616836 | tf_op jit(solution)/shard_map/while/body/eval_jaxpr/div | solution.py:60
  141.0 8.4 %multiply_reduce_fusion.2 = f32[4096]{0:T(1024)S(1)} fusion(f32[4,128,4096]{1,2,0:T(8,128)} %fusion.72, f32[128]{0:T(128)S(1)} %compare_convert_fusion.3, pred[128,4096]{0,1:T(8,128)(4,1)S(1)} %compare_and_fusion.2, bf16[128,4,128]{0,2,1:T(8,128)(2,1)S(1)} %bitcast.70, bf16[4096,1024]{1,0:T(8,128)(2,1)} %get-tuple-element.300, s32[]{:T(128)S(6)} %select_n.79), kind=kOutput, calls=%fused_computation.5.clone.1 | convolution fusion | flops 551551488 | bytes 10633732 | tf_op jit(solution)/shard_map/while/body/eval_jaxpr/sub | solution.py:58
  149.3 1.6 dynamic_update_slice.13
  151.0 1.3 compare_convert_fusion.3
  152.3 1.4 compare_and_fusion.2
  153.7 8.6 %fusion.72 = f32[4,128,4096]{1,2,0:T(8,128)} fusion(pred[128,4096]{0,1:T(8,128)(4,1)S(1)} %compare_and_fusion.2, bf16[128,4,128]{0,2,1:T(8,128)(2,1)S(1)} %bitcast.69, bf16[4096,1024]{1,0:T(8,128)(2,1)} %get-tuple-element.300, s32[]{:T(128)S(6)} %select_n.79), kind=kOutput, calls=%fused_computation.2.clone.1 | convolution fusion | flops 545268736 | bytes 10616836 | tf_op jit(solution)/shard_map/while/body/eval_jaxpr/div | solution.py:60
  162.3 8.4 %multiply_reduce_fusion.2 = f32[4096]{0:T(1024)S(1)} fusion(f32[4,128,4096]{1,2,0:T(8,128)} %fusion.72, f32[128]{0:T(128)S(1)} %compare_convert_fusion.3, pred[128,4096]{0,1:T(8,128)(4,1)S(1)} %compare_and_fusion.2, bf16[128,4,128]{0,2,1:T(8,128)(2,1)S(1)} %bitcast.70, bf16[4096,1024]{1,0:T(8,128)(2,1)} %get-tuple-element.300, s32[]{:T(128)S(6)} %select_n.79), kind=kOutput, calls=%fused_computation.5.clone.1 | convolution fusion | flops 551551488 | bytes 10633732 | tf_op jit(solution)/shard_map/while/body/eval_jaxpr/sub | solution.py:58
  170.7 1.6 dynamic_update_slice.13
  172.3 1.3 compare_convert_fusion.3
  173.6 1.4 compare_and_fusion.2
  175.0 8.6 %fusion.72 = f32[4,128,4096]{1,2,0:T(8,128)} fusion(pred[128,4096]{0,1:T(8,128)(4,1)S(1)} %compare_and_fusion.2, bf16[128,4,128]{0,2,1:T(8,128)(2,1)S(1)} %bitcast.69, bf16[4096,1024]{1,0:T(8,128)(2,1)} %get-tuple-element.300, s32[]{:T(128)S(6)} %select_n.79), kind=kOutput, calls=%fused_computation.2.clone.1 | convolution fusion | flops 545268736 | bytes 10616836 | tf_op jit(solution)/shard_map/while/body/eval_jaxpr/div | solution.py:60
  183.6 8.4 %multiply_reduce_fusion.2 = f32[4096]{0:T(1024)S(1)} fusion(f32[4,128,4096]{1,2,0:T(8,128)} %fusion.72, f32[128]{0:T(128)S(1)} %compare_convert_fusion.3, pred[128,4096]{0,1:T(8,128)(4,1)S(1)} %compare_and_fusion.2, bf16[128,4,128]{0,2,1:T(8,128)(2,1)S(1)} %bitcast.70, bf16[4096,1024]{1,0:T(8,128)(2,1)} %get-tuple-element.300, s32[]{:T(128)S(6)} %select_n.79), kind=kOutput, calls=%fused_computation.5.clone.1 | convolution fusion | flops 551551488 | bytes 10633732 | tf_op jit(solution)/shard_map/while/body/eval_jaxpr/sub | solution.py:58
  192.0 1.6 dynamic_update_slice.13
  193.6 1.3 compare_convert_fusion.3
  194.9 1.4 compare_and_fusion.2
  196.3 8.6 %fusion.72 = f32[4,128,4096]{1,2,0:T(8,128)} fusion(pred[128,4096]{0,1:T(8,128)(4,1)S(1)} %compare_and_fusion.2, bf16[128,4,128]{0,2,1:T(8,128)(2,1)S(1)} %bitcast.69, bf16[4096,1024]{1,0:T(8,128)(2,1)} %get-tuple-element.300, s32[]{:T(128)S(6)} %select_n.79), kind=kOutput, calls=%fused_computation.2.clone.1 | convolution fusion | flops 545268736 | bytes 10616836 | tf_op jit(solution)/shard_map/while/body/eval_jaxpr/div | solution.py:60
  204.9 8.4 %multiply_reduce_fusion.2 = f32[4096]{0:T(1024)S(1)} fusion(f32[4,128,4096]{1,2,0:T(8,128)} %fusion.72, f32[128]{0:T(128)S(1)} %compare_convert_fusion.3, pred[128,4096]{0,1:T(8,128)(4,1)S(1)} %compare_and_fusion.2, bf16[128,4,128]{0,2,1:T(8,128)(2,1)S(1)} %bitcast.70, bf16[4096,1024]{1,0:T(8,128)(2,1)} %get-tuple-element.300, s32[]{:T(128)S(6)} %select_n.79), kind=kOutput, calls=%fused_computation.5.clone.1 | convolution fusion | flops 551551488 | bytes 10633732 | tf_op jit(solution)/shard_map/while/body/eval_jaxpr/sub | solution.py:58
  213.3 1.6 dynamic_update_slice.13
  214.9 1.3 compare_convert_fusion.3
  216.2 1.4 compare_and_fusion.2
  217.6 8.6 %fusion.72 = f32[4,128,4096]{1,2,0:T(8,128)} fusion(pred[128,4096]{0,1:T(8,128)(4,1)S(1)} %compare_and_fusion.2, bf16[128,4,128]{0,2,1:T(8,128)(2,1)S(1)} %bitcast.69, bf16[4096,1024]{1,0:T(8,128)(2,1)} %get-tuple-element.300, s32[]{:T(128)S(6)} %select_n.79), kind=kOutput, calls=%fused_computation.2.clone.1 | convolution fusion | flops 545268736 | bytes 10616836 | tf_op jit(solution)/shard_map/while/body/eval_jaxpr/div | solution.py:60
  226.2 8.4 %multiply_reduce_fusion.2 = f32[4096]{0:T(1024)S(1)} fusion(f32[4,128,4096]{1,2,0:T(8,128)} %fusion.72, f32[128]{0:T(128)S(1)} %compare_convert_fusion.3, pred[128,4096]{0,1:T(8,128)(4,1)S(1)} %compare_and_fusion.2, bf16[128,4,128]{0,2,1:T(8,128)(2,1)S(1)} %bitcast.70, bf16[4096,1024]{1,0:T(8,128)(2,1)} %get-tuple-element.300, s32[]{:T(128)S(6)} %select_n.79), kind=kOutput, calls=%fused_computation.5.clone.1 | convolution fusion | flops 551551488 | bytes 10633732 | tf_op jit(solution)/shard_map/while/body/eval_jaxpr/sub | solution.py:58
  234.6 1.6 dynamic_update_slice.13
  236.2 5.5 %all-to-all-start = ((f32[32,8,128]{2,1,0:T(8,128)}), f32[32,8,128]{2,1,0:T(8,128)S(1)}, u32[]{:S(2)}, u32[]{:S(2)}) async-start(f32[32,8,128]{2,1,0:T(8,128)} %bitcast.9), calls=%async_computation | async-start | bytes 262144 | tf_op jit(solution)/shard_map/all_to_all | solution.py:15
  242.0 6.5 %multiply_convert_fusion = (bf16[128,1024]{1,0:T(8,128)(2,1)S(1)}, f32[128,1024]{1,0:T(8,128)S(1)}) fusion(f32[1024]{0:T(1024)S(1)} %copy-done.1, bf16[6144,1024]{1,0:T(8,128)(2,1)} %param.16, bf16[128,1024]{0,1:T(8,128)(2,1)S(1)} %bitcast.73, bf16[128,1024]{0,1:T(8,128)(2,1)S(1)} %bitcast.71, bf16[128,4096]{0,1:T(8,128)(2,1)S(1)} %get-tuple-element.317), kind=kOutput, calls=%fused_computation.42 | convolution fusion | flops 1616117760 | bytes 14946304 | tf_op jit(solution)/shard_map/dot_general | solution.py:70
  248.5 0.7 compare_convert_fusion.1
  249.1 0.4 all-to-all-done
  249.6 0.3 convert_reduce_fusion.1
  249.9 0.4 convert_reduce_fusion
  250.3 13.2 %fusion.46 = f32[6144,1024]{1,0:T(8,128)} fusion(bf16[128,1024]{1,0:T(8,128)(2,1)S(1)} %get-tuple-element.212, bf16[128,1024]{0,1:T(8,128)(2,1)S(1)} %bitcast.74, bf16[128,1024]{0,1:T(8,128)(2,1)S(1)} %bitcast.72, bf16[128,4096]{0,1:T(8,128)(2,1)S(1)} %get-tuple-element.317), kind=kOutput, calls=%fused_computation.40 | convolution fusion | flops 1615331328 | bytes 27000832 | tf_op jit(solution)/shard_map/dot_general | solution.py:92
  263.5 0.2 fusion.52
  263.8 0.3 reshape.87
  264.1 67.0 %psum.7 = f32[9224]{0:T(1024)S(1)} all-reduce(f32[9224]{0:T(1024)S(1)} %pad_maximum_fusion.3), channel_id=1, replica_groups=mesh['seq'=32,'batch'=4] {'seq','batch'}, use_global_device_ids=true, to_apply=%region_9.10 | all-reduce | flops 9224 | bytes 73792 | tf_op jit(solution)/shard_map/psum | solution.py:23
  331.0 0.5 slice.22
  331.5 0.6 slice.20
  332.1 0.3 reshape.88
  332.4 0.8 copy.18
  333.2 178.8 %reduce-scatter.2.cloned.1.call-done = f32[48,1024]{1,0:T(8,128)} async-done(((f32[6144,1024]{1,0:T(8,128)}), f32[48,1024]{1,0:T(8,128)}) %reduce-scatter.2.cloned.1.call-update) | async-done | bytes 196624 | tf_op jit(solution)/shard_map/reduce_scatter | solution.py:91
  (23 shorter events, 0.6 us)
Async XLA Ops:
  7.2 242.5 %copy-start = (bf16[1024,8]{0,1:T(8,128)(2,1)S(1)}, bf16[1024,8]{0,1:T(8,128)(2,1)}, u32[]{:S(2)}) copy-start(bf16[1024,8]{0,1:T(8,128)(2,1)} %param.18) | copy-start | bytes 49156
  7.2 58.5 %all-gather.3.cloned.1.call-start = ((), (), s32[]{:S(2)}) async-start(), calls=%async_computation.3 | async-start | bytes 8650752 | tf_op jit(solution)/shard_map/all_gather | solution.py:36
  65.7 176.3 %copy-start.1 = (f32[1024]{0:T(1024)S(1)}, f32[1024]{0:T(1024)}, u32[]{:S(2)}) copy-start(f32[1024]{0:T(1024)} %param.17) | copy-start | bytes 12292
  236.2 13.3 %all-to-all-start = ((f32[32,8,128]{2,1,0:T(8,128)}), f32[32,8,128]{2,1,0:T(8,128)S(1)}, u32[]{:S(2)}, u32[]{:S(2)}) async-start(f32[32,8,128]{2,1,0:T(8,128)} %bitcast.9), calls=%async_computation | async-start | bytes 262144 | tf_op jit(solution)/shard_map/all_to_all | solution.py:15
  241.7 270.2 %reduce-scatter.2.cloned.1.call-start = ((), (), s32[]{:S(2)}) async-start(), calls=%async_computation.2 | async-start | bytes 25362432 | tf_op jit(solution)/shard_map/reduce_scatter | solution.py:91
  242.0 7.6 %copy-start.2 = (f32[8]{0:T(128)S(1)}, f32[8]{0:T(128)}, u32[]{:S(2)}) copy-start(f32[8]{0:T(128)} %param.19) | copy-start | bytes 100
Sparse Core Ops, SparseCore 0:
  10.3 55.3 all-gather.2
  263.7 248.2 reduce-scatter.1
where the time goes:
time: 520 us; the launch traced here: 519 us
  waiting for transfers between devices  230 us (44%)
  matrix products  156 us (30%)
  blocking collectives  67 us (13%)
  other arithmetic  24.9 us (5%)
  local copies, waits for them, and re-layouts  19.4 us (4%)
  between operations  14.8 us (3%)
  starting transfers between devices  5.76 us (1%)
    reduce_scatter x1, waiting for transfers between devices, on_device(): lax.psum_scatter(lax.dot_general(features, delta, (((0,), (0,)), ((), ())...  179 us
    div x8, matrix products, group_mass(): share = weights / denom * query_live[None, :, None]  68.8 us
    sub x8, matrix products, group_mass(): weights = jnp.where(allowed[None], jnp.exp(masked - top), 0.0)  67 us
    psum x1, blocking collectives, in_one(): so_far = lax.psum(jnp.concatenate([a.ravel() for a in arrays]), axis)  67 us
    all_gather x1, waiting for transfers between devices, on_device(): every_key = lax.all_gather(k_rows, 'seq', axis=0, tiled=True)  50.5 us
    dot_general x1, matrix products, on_device(): lax.dot_general(features, delta, (((0,), (0,)), ((), ())), preferred_elem...  13.2 us
    dynamic_update_slice x8, local copies, waits for them, and re-layouts, group_mass(): return lax.dynamic_update_index_in_dim(sums, column, index, 0)  12.9 us
    and x8, other arithmetic, on_device(): (key_pos[None, :] <= query_pos[:, None]) & (key_pos < limit)[None, :]  11.1 us
  transfers between devices with their start and end apart: 3, of which 3 were waited for; matrix products, arithmetic and copies ran while one was open for 3% of the time, Pallas kernels for 0%

commit v1 on v0

--- a/solution.py
+++ b/solution.py
@@ -33,7 +33,9 @@
     head_size = k_rows.shape[1] // heads_kv
     group_index = q_rows.shape[1] // k_rows.shape[1]
     scale = 1.0 / math.sqrt(head_size)
-    every_key = lax.all_gather(k_rows, "seq", axis=0, tiled=True)
+    every_key = jnp.concatenate(
+        lax.all_to_all(jnp.stack([k_rows] * lax.axis_size("seq")), "seq", 0, 0), axis=0
+    )
     total = every_key.shape[0]
     order = block_pos[0]
     offsets = jnp.arange(rows, dtype=jnp.int32)

time: 520 us -> 598 us (1.15)
  waiting for transfers between devices: 230 us -> 290 us
  starting transfers between devices: 5.76 us -> 23 us
    all_to_all x0 -> x1, waiting for transfers between devices: none -> 110 us  [on_device(): lax.all_to_all(jnp.stack([k_rows] * lax.axis_size('seq')), 'seq', 0, 0)]
    all_gather x1 -> x0, waiting for transfers between devices: 50.5 us -> none  [on_device(): every_key = lax.all_gather(k_rows, 'seq', axis=0, tiled=True)]
    all_to_all x0 -> x1, starting transfers between devices: none -> 8.72 us  [on_device(): lax.all_to_all(jnp.stack([k_rows] * lax.axis_size('seq')), 'seq', 0, 0)]
    all_to_all x1, starting transfers between devices: 5.5 us -> 14 us  [sent_and_summed(): tiles = lax.all_to_all(split_up(array, dim, size), axis, 0, 0, tiled=True)]
  transfers between devices with their start and end apart: 3 -> 3, of which waited for: 3 -> 3; matrix products, arithmetic and copies ran while one was open for 3% -> 2% of each run, Pallas kernels for 0% -> 0%
where the time goes in v1:
time: 598 us; the launch traced here: 597 us
  waiting for transfers between devices  290 us (48%)
  matrix products  156 us (26%)
  blocking collectives  67 us (11%)
  other arithmetic  23.6 us (4%)
  starting transfers between devices  23 us (4%)
  local copies, waits for them, and re-layouts  21.8 us (4%)
  between operations  14.9 us (2%)
    reduce_scatter x1, waiting for transfers between devices, on_device(): lax.psum_scatter(lax.dot_general(features, delta, (((0,), (0,)), ((), ())...  179 us
    all_to_all x1, waiting for transfers between devices, on_device(): lax.all_to_all(jnp.stack([k_rows] * lax.axis_size('seq')), 'seq', 0, 0)  110 us
    div x8, matrix products, group_mass(): share = weights / denom * query_live[None, :, None]  68.8 us
    psum x1, blocking collectives, in_one(): so_far = lax.psum(jnp.concatenate([a.ravel() for a in arrays]), axis)  67 us
    sub x8, matrix products, group_mass(): weights = jnp.where(allowed[None], jnp.exp(masked - top), 0.0)  67 us
    all_to_all x1, starting transfers between devices, sent_and_summed(): tiles = lax.all_to_all(split_up(array, dim, size), axis, 0, 0, tiled=True)  14 us
    dot_general x1, matrix products, on_device(): lax.dot_general(features, delta, (((0,), (0,)), ((), ())), preferred_elem...  13.2 us
    dynamic_update_slice x8, local copies, waits for them, and re-layouts, group_mass(): return lax.dynamic_update_index_in_dim(sums, column, index, 0)  12.9 us
  transfers between devices with their start and end apart: 3, of which 3 were waited for; matrix products, arithmetic and copies ran while one was open for 2% of the time, Pallas kernels for 0%

profile of v1, /device:TPU:0, one launch (start us, length us, event | category | flops | bytes accessed | tf_op | source)
XLA Modules:
  0.0 596.5 jit_solution(11090086855176707046)
XLA Ops:
  7.2 5.2 stack.3
  12.4 8.7 %all-to-all-start = ((bf16[32,128,1024]{2,1,0:T(8,128)(2,1)}), bf16[32,128,1024]{2,1,0:T(8,128)(2,1)}, u32[]{:S(2)}, u32[]{:S(2)}) async-start(bf16[32,128,1024]{2,1,0:T(8,128)(2,1)} %stack.3), calls=%async_computation | async-start | bytes 16777216 | tf_op jit(solution)/shard_map/all_to_all | solution.py:37
  21.2 0.2 copy.15
  22.2 0.7 copy.14
  22.9 0.6 fusion.51
  23.5 0.6 iota_add_fusion
  24.3 110.4 %all-to-all-done = bf16[32,128,1024]{2,1,0:T(8,128)(2,1)} async-done(((bf16[32,128,1024]{2,1,0:T(8,128)(2,1)}), bf16[32,128,1024]{2,1,0:T(8,128)(2,1)}, u32[]{:S(2)}, u32[]{:S(2)}) %all-to-all-start) | async-done | bytes 8388640 | tf_op jit(solution)/shard_map/all_to_all | solution.py:37
  134.7 170.6 %while.16 = (s32[]{:T(128)}, f32[8,4096]{1,0:T(8,128)}, bf16[4096,1024]{1,0:T(8,128)(2,1)}, bf16[128,4096]{0,1:T(8,128)(2,1)S(1)}, s32[128]{0:T(128)S(1)}, /*ind...) while((s32[]{:T(128)}, f32[8,4096]{1,0:T(8,128)}, ...), condition=%wide.region_4.5_spmd.clone, body=%wide.region_0.4_spmd.clone.sunk | while | flops 1097869184 | bytes 22091528 | solution.py:66
  134.7 1.3 compare_convert_fusion.3
  136.0 1.4 compare_and_fusion.2
  137.4 8.6 %fusion.72 = f32[4,128,4096]{1,2,0:T(8,128)} fusion(pred[128,4096]{0,1:T(8,128)(4,1)S(1)} %compare_and_fusion.2, bf16[128,4,128]{0,2,1:T(8,128)(2,1)S(1)} %bitcast.70, bf16[4096,1024]{1,0:T(8,128)(2,1)} %get-tuple-element.300, s32[]{:T(128)S(6)} %select_n.79), kind=kOutput, calls=%fused_computation.2.clone.1 | convolution fusion | flops 545268736 | bytes 10616836 | tf_op jit(solution)/shard_map/while/body/eval_jaxpr/div | solution.py:62
  146.0 8.4 %multiply_reduce_fusion.2 = f32[4096]{0:T(1024)S(1)} fusion(f32[4,128,4096]{1,2,0:T(8,128)} %fusion.72, f32[128]{0:T(128)S(1)} %compare_convert_fusion.3, pred[128,4096]{0,1:T(8,128)(4,1)S(1)} %compare_and_fusion.2, bf16[128,4,128]{0,2,1:T(8,128)(2,1)S(1)} %bitcast.71, bf16[4096,1024]{1,0:T(8,128)(2,1)} %get-tuple-element.300, s32[]{:T(128)S(6)} %select_n.79), kind=kOutput, calls=%fused_computation.5.clone.1 | convolution fusion | flops 551551488 | bytes 10633732 | tf_op jit(solution)/shard_map/while/body/eval_jaxpr/sub | solution.py:60
  154.4 1.6 dynamic_update_slice.13
  156.0 1.3 compare_convert_fusion.3
  157.3 1.4 compare_and_fusion.2
  158.7 8.6 %fusion.72 = f32[4,128,4096]{1,2,0:T(8,128)} fusion(pred[128,4096]{0,1:T(8,128)(4,1)S(1)} %compare_and_fusion.2, bf16[128,4,128]{0,2,1:T(8,128)(2,1)S(1)} %bitcast.70, bf16[4096,1024]{1,0:T(8,128)(2,1)} %get-tuple-element.300, s32[]{:T(128)S(6)} %select_n.79), kind=kOutput, calls=%fused_computation.2.clone.1 | convolution fusion | flops 545268736 | bytes 10616836 | tf_op jit(solution)/shard_map/while/body/eval_jaxpr/div | solution.py:62
  167.3 8.4 %multiply_reduce_fusion.2 = f32[4096]{0:T(1024)S(1)} fusion(f32[4,128,4096]{1,2,0:T(8,128)} %fusion.72, f32[128]{0:T(128)S(1)} %compare_convert_fusion.3, pred[128,4096]{0,1:T(8,128)(4,1)S(1)} %compare_and_fusion.2, bf16[128,4,128]{0,2,1:T(8,128)(2,1)S(1)} %bitcast.71, bf16[4096,1024]{1,0:T(8,128)(2,1)} %get-tuple-element.300, s32[]{:T(128)S(6)} %select_n.79), kind=kOutput, calls=%fused_computation.5.clone.1 | convolution fusion | flops 551551488 | bytes 10633732 | tf_op jit(solution)/shard_map/while/body/eval_jaxpr/sub | solution.py:60
  175.7 1.6 dynamic_update_slice.13
  177.3 1.3 compare_convert_fusion.3
  178.7 1.4 compare_and_fusion.2
  180.1 8.6 %fusion.72 = f32[4,128,4096]{1,2,0:T(8,128)} fusion(pred[128,4096]{0,1:T(8,128)(4,1)S(1)} %compare_and_fusion.2, bf16[128,4,128]{0,2,1:T(8,128)(2,1)S(1)} %bitcast.70, bf16[4096,1024]{1,0:T(8,128)(2,1)} %get-tuple-element.300, s32[]{:T(128)S(6)} %select_n.79), kind=kOutput, calls=%fused_computation.2.clone.1 | convolution fusion | flops 545268736 | bytes 10616836 | tf_op jit(solution)/shard_map/while/body/eval_jaxpr/div | solution.py:62
  188.7 8.4 %multiply_reduce_fusion.2 = f32[4096]{0:T(1024)S(1)} fusion(f32[4,128,4096]{1,2,0:T(8,128)} %fusion.72, f32[128]{0:T(128)S(1)} %compare_convert_fusion.3, pred[128,4096]{0,1:T(8,128)(4,1)S(1)} %compare_and_fusion.2, bf16[128,4,128]{0,2,1:T(8,128)(2,1)S(1)} %bitcast.71, bf16[4096,1024]{1,0:T(8,128)(2,1)} %get-tuple-element.300, s32[]{:T(128)S(6)} %select_n.79), kind=kOutput, calls=%fused_computation.5.clone.1 | convolution fusion | flops 551551488 | bytes 10633732 | tf_op jit(solution)/shard_map/while/body/eval_jaxpr/sub | solution.py:60
  197.0 1.6 dynamic_update_slice.13
  198.6 1.3 compare_convert_fusion.3
  200.0 1.4 compare_and_fusion.2
  201.4 8.6 %fusion.72 = f32[4,128,4096]{1,2,0:T(8,128)} fusion(pred[128,4096]{0,1:T(8,128)(4,1)S(1)} %compare_and_fusion.2, bf16[128,4,128]{0,2,1:T(8,128)(2,1)S(1)} %bitcast.70, bf16[4096,1024]{1,0:T(8,128)(2,1)} %get-tuple-element.300, s32[]{:T(128)S(6)} %select_n.79), kind=kOutput, calls=%fused_computation.2.clone.1 | convolution fusion | flops 545268736 | bytes 10616836 | tf_op jit(solution)/shard_map/while/body/eval_jaxpr/div | solution.py:62
  210.0 8.4 %multiply_reduce_fusion.2 = f32[4096]{0:T(1024)S(1)} fusion(f32[4,128,4096]{1,2,0:T(8,128)} %fusion.72, f32[128]{0:T(128)S(1)} %compare_convert_fusion.3, pred[128,4096]{0,1:T(8,128)(4,1)S(1)} %compare_and_fusion.2, bf16[128,4,128]{0,2,1:T(8,128)(2,1)S(1)} %bitcast.71, bf16[4096,1024]{1,0:T(8,128)(2,1)} %get-tuple-element.300, s32[]{:T(128)S(6)} %select_n.79), kind=kOutput, calls=%fused_computation.5.clone.1 | convolution fusion | flops 551551488 | bytes 10633732 | tf_op jit(solution)/shard_map/while/body/eval_jaxpr/sub | solution.py:60
  218.4 1.6 dynamic_update_slice.13
  220.0 1.3 compare_convert_fusion.3
  221.3 1.4 compare_and_fusion.2
  222.7 8.6 %fusion.72 = f32[4,128,4096]{1,2,0:T(8,128)} fusion(pred[128,4096]{0,1:T(8,128)(4,1)S(1)} %compare_and_fusion.2, bf16[128,4,128]{0,2,1:T(8,128)(2,1)S(1)} %bitcast.70, bf16[4096,1024]{1,0:T(8,128)(2,1)} %get-tuple-element.300, s32[]{:T(128)S(6)} %select_n.79), kind=kOutput, calls=%fused_computation.2.clone.1 | convolution fusion | flops 545268736 | bytes 10616836 | tf_op jit(solution)/shard_map/while/body/eval_jaxpr/div | solution.py:62
  231.3 8.4 %multiply_reduce_fusion.2 = f32[4096]{0:T(1024)S(1)} fusion(f32[4,128,4096]{1,2,0:T(8,128)} %fusion.72, f32[128]{0:T(128)S(1)} %compare_convert_fusion.3, pred[128,4096]{0,1:T(8,128)(4,1)S(1)} %compare_and_fusion.2, bf16[128,4,128]{0,2,1:T(8,128)(2,1)S(1)} %bitcast.71, bf16[4096,1024]{1,0:T(8,128)(2,1)} %get-tuple-element.300, s32[]{:T(128)S(6)} %select_n.79), kind=kOutput, calls=%fused_computation.5.clone.1 | convolution fusion | flops 551551488 | bytes 10633732 | tf_op jit(solution)/shard_map/while/body/eval_jaxpr/sub | solution.py:60
  239.7 1.6 dynamic_update_slice.13
  241.3 1.3 compare_convert_fusion.3
  242.6 1.4 compare_and_fusion.2
  244.0 8.6 %fusion.72 = f32[4,128,4096]{1,2,0:T(8,128)} fusion(pred[128,4096]{0,1:T(8,128)(4,1)S(1)} %compare_and_fusion.2, bf16[128,4,128]{0,2,1:T(8,128)(2,1)S(1)} %bitcast.70, bf16[4096,1024]{1,0:T(8,128)(2,1)} %get-tuple-element.300, s32[]{:T(128)S(6)} %select_n.79), kind=kOutput, calls=%fused_computation.2.clone.1 | convolution fusion | flops 545268736 | bytes 10616836 | tf_op jit(solution)/shard_map/while/body/eval_jaxpr/div | solution.py:62
  252.6 8.4 %multiply_reduce_fusion.2 = f32[4096]{0:T(1024)S(1)} fusion(f32[4,128,4096]{1,2,0:T(8,128)} %fusion.72, f32[128]{0:T(128)S(1)} %compare_convert_fusion.3, pred[128,4096]{0,1:T(8,128)(4,1)S(1)} %compare_and_fusion.2, bf16[128,4,128]{0,2,1:T(8,128)(2,1)S(1)} %bitcast.71, bf16[4096,1024]{1,0:T(8,128)(2,1)} %get-tuple-element.300, s32[]{:T(128)S(6)} %select_n.79), kind=kOutput, calls=%fused_computation.5.clone.1 | convolution fusion | flops 551551488 | bytes 10633732 | tf_op jit(solution)/shard_map/while/body/eval_jaxpr/sub | solution.py:60
  261.0 1.6 dynamic_update_slice.13
  262.6 1.3 compare_convert_fusion.3
  263.9 1.4 compare_and_fusion.2
  265.3 8.6 %fusion.72 = f32[4,128,4096]{1,2,0:T(8,128)} fusion(pred[128,4096]{0,1:T(8,128)(4,1)S(1)} %compare_and_fusion.2, bf16[128,4,128]{0,2,1:T(8,128)(2,1)S(1)} %bitcast.70, bf16[4096,1024]{1,0:T(8,128)(2,1)} %get-tuple-element.300, s32[]{:T(128)S(6)} %select_n.79), kind=kOutput, calls=%fused_computation.2.clone.1 | convolution fusion | flops 545268736 | bytes 10616836 | tf_op jit(solution)/shard_map/while/body/eval_jaxpr/div | solution.py:62
  273.9 8.4 %multiply_reduce_fusion.2 = f32[4096]{0:T(1024)S(1)} fusion(f32[4,128,4096]{1,2,0:T(8,128)} %fusion.72, f32[128]{0:T(128)S(1)} %compare_convert_fusion.3, pred[128,4096]{0,1:T(8,128)(4,1)S(1)} %compare_and_fusion.2, bf16[128,4,128]{0,2,1:T(8,128)(2,1)S(1)} %bitcast.71, bf16[4096,1024]{1,0:T(8,128)(2,1)} %get-tuple-element.300, s32[]{:T(128)S(6)} %select_n.79), kind=kOutput, calls=%fused_computation.5.clone.1 | convolution fusion | flops 551551488 | bytes 10633732 | tf_op jit(solution)/shard_map/while/body/eval_jaxpr/sub | solution.py:60
  282.3 1.6 dynamic_update_slice.13
  283.9 1.3 compare_convert_fusion.3
  285.3 1.4 compare_and_fusion.2
  286.7 8.6 %fusion.72 = f32[4,128,4096]{1,2,0:T(8,128)} fusion(pred[128,4096]{0,1:T(8,128)(4,1)S(1)} %compare_and_fusion.2, bf16[128,4,128]{0,2,1:T(8,128)(2,1)S(1)} %bitcast.70, bf16[4096,1024]{1,0:T(8,128)(2,1)} %get-tuple-element.300, s32[]{:T(128)S(6)} %select_n.79), kind=kOutput, calls=%fused_computation.2.clone.1 | convolution fusion | flops 545268736 | bytes 10616836 | tf_op jit(solution)/shard_map/while/body/eval_jaxpr/div | solution.py:62
  295.3 8.4 %multiply_reduce_fusion.2 = f32[4096]{0:T(1024)S(1)} fusion(f32[4,128,4096]{1,2,0:T(8,128)} %fusion.72, f32[128]{0:T(128)S(1)} %compare_convert_fusion.3, pred[128,4096]{0,1:T(8,128)(4,1)S(1)} %compare_and_fusion.2, bf16[128,4,128]{0,2,1:T(8,128)(2,1)S(1)} %bitcast.71, bf16[4096,1024]{1,0:T(8,128)(2,1)} %get-tuple-element.300, s32[]{:T(128)S(6)} %select_n.79), kind=kOutput, calls=%fused_computation.5.clone.1 | convolution fusion | flops 551551488 | bytes 10633732 | tf_op jit(solution)/shard_map/while/body/eval_jaxpr/sub | solution.py:60
  303.6 1.6 dynamic_update_slice.13
  305.3 14.0 %all-to-all-start.1 = ((f32[32,8,128]{2,1,0:T(8,128)}), f32[32,8,128]{2,1,0:T(8,128)S(1)}, u32[]{:S(2)}, u32[]{:S(2)}) async-start(f32[32,8,128]{2,1,0:T(8,128)} %bitcast.10), calls=%async_computation.1 | async-start | bytes 262144 | tf_op jit(solution)/shard_map/all_to_all | solution.py:15
  319.3 0.2 reduce-scatter.2.cloned.1.call-start
  319.6 6.5 %multiply_convert_fusion = (bf16[128,1024]{1,0:T(8,128)(2,1)S(1)}, f32[128,1024]{1,0:T(8,128)S(1)}) fusion(f32[1024]{0:T(1024)S(1)} %copy-done.4, bf16[6144,1024]{1,0:T(8,128)(2,1)} %param.16, bf16[128,1024]{0,1:T(8,128)(2,1)S(1)} %bitcast.74, bf16[128,1024]{0,1:T(8,128)(2,1)S(1)} %bitcast.72, bf16[128,4096]{0,1:T(8,128)(2,1)S(1)} %get-tuple-element.318), kind=kOutput, calls=%fused_computation.42 | convolution fusion | flops 1616117760 | bytes 14946304 | tf_op jit(solution)/shard_map/dot_general | solution.py:72
  326.1 0.7 compare_convert_fusion.1
  326.7 0.4 all-to-all-done.1
  327.2 0.3 convert_reduce_fusion.1
  327.5 0.4 convert_reduce_fusion
  327.9 13.2 %fusion.46 = f32[6144,1024]{1,0:T(8,128)} fusion(bf16[128,1024]{1,0:T(8,128)(2,1)S(1)} %get-tuple-element.212, bf16[128,1024]{0,1:T(8,128)(2,1)S(1)} %bitcast.75, bf16[128,1024]{0,1:T(8,128)(2,1)S(1)} %bitcast.73, bf16[128,4096]{0,1:T(8,128)(2,1)S(1)} %get-tuple-element.318), kind=kOutput, calls=%fused_computation.40 | convolution fusion | flops 1615331328 | bytes 27000832 | tf_op jit(solution)/shard_map/dot_general | solution.py:94
  341.1 0.3 fusion.52
  341.4 0.3 reshape.92
  341.6 67.0 %psum.7 = f32[9224]{0:T(1024)S(1)} all-reduce(f32[9224]{0:T(1024)S(1)} %pad_maximum_fusion.3), channel_id=1, replica_groups=mesh['seq'=32,'batch'=4] {'seq','batch'}, use_global_device_ids=true, to_apply=%region_9.10 | all-reduce | flops 9224 | bytes 73792 | tf_op jit(solution)/shard_map/psum | solution.py:23
  408.6 0.5 slice.22
  409.2 0.6 slice.20
  409.7 0.3 reshape.93
  410.0 0.8 copy.19
  410.8 178.8 %reduce-scatter.2.cloned.1.call-done = f32[48,1024]{1,0:T(8,128)} async-done(((f32[6144,1024]{1,0:T(8,128)}), f32[48,1024]{1,0:T(8,128)}) %reduce-scatter.2.cloned.1.call-update) | async-done | bytes 196624 | tf_op jit(solution)/shard_map/reduce_scatter | solution.py:93
  (31 shorter events, 0.6 us)
Async XLA Ops:
  7.2 320.0 %copy-start = (bf16[1024,8]{0,1:T(8,128)(2,1)S(1)}, bf16[1024,8]{0,1:T(8,128)(2,1)}, u32[]{:S(2)}) copy-start(bf16[1024,8]{0,1:T(8,128)(2,1)} %param.18) | copy-start | bytes 49156
  12.4 8.8 %copy-start.1 = (bf16[1,128,1024]{2,1,0:T(8,128)(2,1)S(1)}, bf16[1,128,1024]{2,1,0:T(8,128)(2,1)}, u32[]{:S(2)}) copy-start(bf16[1,128,1024]{2,1,0:T(8,128)(2,1)} %param.12) | copy-start | bytes 786436
  12.4 9.6 %copy-start.3 = (bf16[1,128,1024]{2,1,0:T(8,128)(2,1)S(1)}, bf16[1,128,1024]{2,1,0:T(8,128)(2,1)}, u32[]{:S(2)}) copy-start(bf16[1,128,1024]{2,1,0:T(8,128)(2,1)} %param.13) | copy-start | bytes 786436
  12.4 9.8 %copy-start.2 = (bf16[1,128,4096]{2,1,0:T(8,128)(2,1)S(1)}, bf16[1,128,4096]{2,1,0:T(8,128)(2,1)}, u32[]{:S(2)}) copy-start(bf16[1,128,4096]{2,1,0:T(8,128)(2,1)} %param.11) | copy-start | bytes 3145732
  12.4 10.5 %copy-start.5 = (s32[1,32]{1,0:T(1,128)S(1)}, s32[1,32]{1,0:T(1,128)}, u32[]{:S(2)}) copy-start(s32[1,32]{1,0:T(1,128)} %param.15) | copy-start | bytes 388
  12.4 122.2 %all-to-all-start = ((bf16[32,128,1024]{2,1,0:T(8,128)(2,1)}), bf16[32,128,1024]{2,1,0:T(8,128)(2,1)}, u32[]{:S(2)}, u32[]{:S(2)}) async-start(bf16[32,128,1024]{2,1,0:T(8,128)(2,1)} %stack.3), calls=%async_computation | async-start | bytes 16777216 | tf_op jit(solution)/shard_map/all_to_all | solution.py:37
  134.7 184.9 %copy-start.4 = (f32[1024]{0:T(1024)S(1)}, f32[1024]{0:T(1024)}, u32[]{:S(2)}) copy-start(f32[1024]{0:T(1024)} %param.17) | copy-start | bytes 12292
  305.3 21.9 %all-to-all-start.1 = ((f32[32,8,128]{2,1,0:T(8,128)}), f32[32,8,128]{2,1,0:T(8,128)S(1)}, u32[]{:S(2)}, u32[]{:S(2)}) async-start(f32[32,8,128]{2,1,0:T(8,128)} %bitcast.10), calls=%async_computation.1 | async-start | bytes 262144 | tf_op jit(solution)/shard_map/all_to_all | solution.py:15
  319.3 270.4 %reduce-scatter.2.cloned.1.call-start = ((), (), s32[]{:S(2)}) async-start(), calls=%async_computation.3 | async-start | bytes 25362432 | tf_op jit(solution)/shard_map/reduce_scatter | solution.py:93
  319.6 7.6 %copy-start.6 = (f32[8]{0:T(128)S(1)}, f32[8]{0:T(128)}, u32[]{:S(2)}) copy-start(f32[8]{0:T(128)} %param.19) | copy-start | bytes 100
Sparse Core Ops, SparseCore 0:
  341.2 248.4 reduce-scatter.1
